TPU v7x, 256 devices: a whole 4x4x8 slice. The times are simulated.
256 devices in a mesh: ctg: 32 (over x, y, core), br: 8 (over z).
Axes of the slice: x: 4, y: 4, z: 8, core: 2. Of those that a mesh axis runs over, the one named last changes fastest.
Arguments:
- base_vm: float32 [10240], P(('ctg', 'br')), may hold values from 0.95 to 1.05
- base_va: float32 [10240], P(('ctg', 'br')), may hold values from -0.6 to 0.6
- delta_state: float32 [256, 2, 10240], P('ctg', None, 'br'), may hold values from -0.18 to 0.18
- multipliers: float32 [256, 2, 10240], P('ctg', None, 'br'), may hold values from -6 to 6
- net_inj: float32 [256, 2, 10240], P('ctg', None, 'br'), may hold values from -6 to 6
- ang_grad: float32 [256, 10240], P('ctg', 'br'), may hold values from -6 to 6
- from_bus: int32 [13312], P('br'), may hold values from 0 to 10239
- to_bus: int32 [13312], P('br'), may hold values from 0 to 10239
- status: int32 [256, 13312], P('ctg', 'br'), may hold values 0 or 1
- conduct: float32 [13312], P('br'), may hold values from 1 to 5
- suscept: float32 [13312], P('br'), may hold values from -15 to -5
- charging: float32 [13312], P('br'), may hold values from 0.1 to 0.6
- rating: float32 [13312], P('br'), may hold values from 1 to 3
- slack: float32 [256, 13312], P('ctg', 'br'), may hold values from 0.05 to 2
- zdual: float32 [256, 13312], P('ctg', 'br'), may hold values from 0.05 to 2
Outputs:
- mismatch: float32 [256, 2, 10240], P('ctg', None, 'br')
- dual_res: float32 [256, 10240], P('ctg', 'br')
- limit_res: float32 [256, 13312], P('ctg', 'br')
- ctg_norms: float32 [256, 4], P('ctg')
- total_norms: float32 [4], replicated
All inputs are finite; a program needn't handle non-finite values. No bound on the sum of `status` on one device may be relied on, other than what follows from the above.
Results may differ from a plain program's by a relative error of at most 0.0003.
Values sent between devices are 32-bit elements; how exact they have to be, the bound alone decides.
A program may use at most 64 MiB of HBM per device.

v0:
```python
import math
import jax
import jax.numpy as jnp
from jax import lax
from jax.sharding import PartitionSpec as P


def turned_gather(arrays, axis, dims):
    turned = [jnp.moveaxis(a, dim, 0) for a, dim in zip(arrays, dims)]
    widths = [t[0].size for t in turned]
    both = jnp.concatenate([t.reshape(-1, w) for t, w in zip(turned, widths)], axis=1)
    whole = lax.all_gather(both, axis, axis=0, tiled=True)
    pieces = jnp.split(whole, [sum(widths[:k]) for k in range(1, len(widths))], axis=1)
    return tuple(
        (
            jnp.moveaxis(b.reshape(-1, *t.shape[1:]), 0, dim)
            for b, t, dim in zip(pieces, turned, dims)
        )
    )


def in_one_piece(arrays, axis, dim, along):
    both = jnp.concatenate(arrays, axis=along)
    whole, at, finished = (lax.all_gather(both, axis, axis=dim, tiled=True), 0, [])
    for a in arrays:
        finished.append(lax.slice_in_dim(whole, at, at + a.shape[along], axis=along))
        at += a.shape[along]
    return tuple(finished)


def in_blocks(array, dim, peers):
    shape = array.shape
    pieces = array.reshape(*shape[:dim], peers, shape[dim] // peers, *shape[dim + 1 :])
    return jnp.moveaxis(pieces, dim, 0)


def summed_on_arrival(array, axis, dim):
    peers = lax.axis_size(axis)
    pieces = lax.all_to_all(in_blocks(array, dim, peers), axis, 0, 0, tiled=True)
    return jnp.sum(pieces, axis=0)


def sent_to_all(array, axis):
    copies = jnp.broadcast_to(array, (lax.axis_size(axis), *array.shape))
    return lax.all_to_all(copies, axis, split_axis=0, concat_axis=0, tiled=True)


def over_copies(array, axis):
    everything = sent_to_all(array, axis)
    return jnp.sum(everything, axis=0)


def in_one(arrays, axis):
    ends = [0]
    for a in arrays:
        ends.append(ends[-1] + a.size)
    subtotal = over_copies(jnp.concatenate([a.ravel() for a in arrays]), axis)
    return tuple((subtotal[b:e].reshape(a.shape) for a, b, e in zip(arrays, ends, ends[1:])))


def block_size(span_total, other_side):
    limit = max(128, (1 << 23) // other_side)
    power = 1 << limit.bit_length() - 1
    return math.gcd(span_total, min(1024, power))


def select_cols(values, index_list):
    row_count, bus_count = values.shape
    col_count = index_list.shape[0]
    span_cols = block_size(bus_count, col_count)
    block_count = bus_count // span_cols
    tiles = values.reshape(row_count, block_count, span_cols).transpose(1, 0, 2)

    def add_block(running, item):
        segment, number = item
        labels = number * span_cols + lax.iota(jnp.int32, span_cols)
        onehot = (labels[:, None] == index_list[None, :]).astype(jnp.float32)
        running = running + jnp.dot(
            segment, onehot, precision=lax.Precision.HIGHEST, preferred_element_type=jnp.float32
        )
        return (running, None)

    start_zero = jnp.zeros((row_count, col_count), jnp.float32)
    numbers = jnp.arange(block_count, dtype=jnp.int32)
    result, _ = lax.scan(add_block, start_zero, (tiles, numbers))
    return result


def spread_rows(values, index_list, bus_count):
    row_count, col_count = values.shape
    span_cols = block_size(bus_count, col_count)
    block_count = bus_count // span_cols

    def one_block(carry, number):
        labels = number * span_cols + lax.iota(jnp.int32, span_cols)
        onehot = (index_list[:, None] == labels[None, :]).astype(jnp.float32)
        piece_sum = jnp.dot(
            values, onehot, precision=lax.Precision.HIGHEST, preferred_element_type=jnp.float32
        )
        return (carry, piece_sum)

    numbers = jnp.arange(block_count, dtype=jnp.int32)
    _, pieces = lax.scan(one_block, jnp.int32(0), numbers)
    return pieces.transpose(1, 0, 2).reshape(row_count, bus_count)


def branch_flows(
    volt_mag, volt_ang, mult_p, mult_q, from_idx, to_idx, conduct, suscept, charging, in_service
):
    scen_count = volt_mag.shape[0]
    stacked = jnp.concatenate([volt_mag, volt_ang, mult_p, mult_q], 0)
    at_from_end = select_cols(stacked, from_idx)
    at_to_end = select_cols(stacked, to_idx)
    volt_from = at_from_end[:scen_count]
    volt_to = at_to_end[:scen_count]
    angle_diff = at_from_end[scen_count : 2 * scen_count] - at_to_end[scen_count : 2 * scen_count]
    mp_from = at_from_end[2 * scen_count : 3 * scen_count]
    mq_from = at_from_end[3 * scen_count :]
    mp_to = at_to_end[2 * scen_count : 3 * scen_count]
    mq_to = at_to_end[3 * scen_count :]
    cos_diff = jnp.cos(angle_diff)
    sin_diff = jnp.sin(angle_diff)
    volt_prod = volt_from * volt_to
    p_from = conduct * volt_from * volt_from - volt_prod * (conduct * cos_diff + suscept * sin_diff)
    q_from = -(suscept + charging) * volt_from * volt_from - volt_prod * (
        conduct * sin_diff - suscept * cos_diff
    )
    p_to = conduct * volt_to * volt_to - volt_prod * (conduct * cos_diff - suscept * sin_diff)
    q_to = -(suscept + charging) * volt_to * volt_to + volt_prod * (
        conduct * sin_diff + suscept * cos_diff
    )
    flow_dual = volt_prod * (
        mp_from * (conduct * sin_diff - suscept * cos_diff)
        - mq_from * (conduct * cos_diff + suscept * sin_diff)
        + mp_to * (conduct * sin_diff + suscept * cos_diff)
        + mq_to * (conduct * cos_diff - suscept * sin_diff)
    )
    at_from = jnp.stack([p_from, q_from, flow_dual], 1) * in_service[:, None, :]
    at_to = jnp.stack([p_to, q_to, -flow_dual], 1) * in_service[:, None, :]
    return (at_from, at_to)


def sum_at_buses(from_vals, to_vals, from_idx, to_idx, offset, bus_count):
    scen_count = from_vals.shape[0]
    both_vals = jnp.concatenate([from_vals, to_vals], 2).reshape(scen_count * 3, -1)
    both_idx = jnp.concatenate([from_idx, to_idx], 0) - offset
    summed = spread_rows(both_vals, both_idx, bus_count)
    return summed.reshape(scen_count, 3, bus_count)


def per_device(
    base_vm,
    base_va,
    delta_state,
    multipliers,
    net_inj,
    ang_grad,
    from_bus,
    to_bus,
    status,
    conduct,
    suscept,
    charging,
    rating,
    slack,
    zdual,
):
    full_vm, full_va = turned_gather((base_vm, base_va), ("ctg", "br"), (0, 0))
    shifts, duals_all = in_one_piece((delta_state, multipliers), "br", 2, 0)
    volt_mag = full_vm[None, :] + shifts[:, 0]
    volt_ang = full_va[None, :] + shifts[:, 1]
    in_service = status.astype(jnp.float32)
    at_from, at_to = branch_flows(
        volt_mag,
        volt_ang,
        duals_all[:, 0],
        duals_all[:, 1],
        from_bus,
        to_bus,
        conduct,
        suscept,
        charging,
        in_service,
    )
    limit_res = in_service * (
        at_from[:, 0] * at_from[:, 0] + at_from[:, 1] * at_from[:, 1] + slack - rating * rating
    )
    complement = in_service * (zdual * slack - 0.01)
    limit_part = jnp.sum(limit_res * limit_res, axis=1)
    comp_part = jnp.sum(complement * complement, axis=1)
    bus_terms = sum_at_buses(at_from, at_to, from_bus, to_bus, 0, shifts.shape[2])
    summed = summed_on_arrival(bus_terms, "br", 2)
    mismatch = summed[:, :2] - net_inj
    dual_res = summed[:, 2] + ang_grad
    mis_part = jnp.sum(mismatch * mismatch, axis=(1, 2))
    dual_part = jnp.sum(dual_res * dual_res, axis=1)
    mis_sq, dual_sq, limit_sq, comp_sq = in_one((mis_part, dual_part, limit_part, comp_part), "br")
    squares = jnp.stack([mis_sq, dual_sq, limit_sq, comp_sq], 1)
    ctg_norms = jnp.sqrt(squares)
    totals = over_copies(jnp.sum(squares, axis=0), "ctg")
    total_norms = jnp.sqrt(totals / (delta_state.shape[0] * lax.axis_size("ctg")))
    return (mismatch, dual_res, limit_res, ctg_norms, total_norms)


def solution(mesh):
    placed = (
        P(("ctg", "br")),
        P(("ctg", "br")),
        P("ctg", None, "br"),
        P("ctg", None, "br"),
        P("ctg", None, "br"),
        P("ctg", "br"),
        P("br"),
        P("br"),
        P("ctg", "br"),
        P("br"),
        P("br"),
        P("br"),
        P("br"),
        P("ctg", "br"),
        P("ctg", "br"),
    )
    return jax.shard_map(
        per_device,
        mesh=mesh,
        in_specs=placed,
        out_specs=(P("ctg", None, "br"), P("ctg", "br"), P("ctg", "br"), P("ctg", None), P()),
        check_vma=False,
    )
```

profile of v0, /device:TPU:1, one launch (start us, length us, event | category | flops | bytes accessed | tf_op | source)
XLA Modules:
  0.0 281.0 jit_solution(867481893369995764)
XLA Ops:
  10.5 67.2 %all-gather = f32[256,40,2]{1,2,0:T(2,128)S(1)} all-gather(f32[1,40,2]{1,2,0:T(2,128)S(1)} %maximum_bitcast_fusion.1), channel_id=1, replica_groups=mesh['ctg'=32,'br'=8] {'ctg','br'}, dimensions={0}, use_global_device_ids=true | all-gather | bytes 82240 | tf_op jit(solution)/shard_map/all_gather | solution.py:12
  79.9 36.7 %while.34 = (s32[]{:T(128)}, f32[32,1664]{1,0:T(8,128)S(1)}, f32[10,32,1024]{2,1,0:T(8,128)S(1)}, s32[10]{0:T(128)S(1)}, s32[1664]{0:T(1024)S(1)}, /*index=5*/s32[]{:T(128)}, s32[1]{0:T(128)}, s32[]{:T(128)}) while((s32[]{:T(128)}, f32[32,1664]{1,0:T(8,128)S(1)}, f32[10,32,1024]{2,1,0:T(8,128)S(1)}, s32[10]{0:T(128)S(1)}, ...), condition=%wide.region_3.4_spmd.clone, body=%wide.region_2.3_spmd.clone.sunk | while | flops 656122880 | bytes 573567 | solution.py:85
  84.8 2.4 fusion.71
  88.5 2.4 fusion.71
  92.2 2.4 fusion.71
  110.5 2.4 fusion.71
  114.2 2.4 fusion.71
  116.6 36.7 %while.33 = (s32[]{:T(128)}, f32[32,1664]{1,0:T(8,128)S(1)}, f32[10,32,1024]{2,1,0:T(8,128)S(1)}, s32[10]{0:T(128)S(1)}, s32[1664]{0:T(1024)S(1)}, /*index=5*/s32[]{:T(128)}, s32[1]{0:T(128)}, s32[]{:T(128)}) while((s32[]{:T(128)}, f32[32,1664]{1,0:T(8,128)S(1)}, f32[10,32,1024]{2,1,0:T(8,128)S(1)}, s32[10]{0:T(128)S(1)}, ...), condition=%wide.region_1.2_spmd.clone, body=%wide.region_0.1_spmd.clone.sunk | while | flops 656122880 | bytes 573567 | solution.py:85
  121.6 2.4 fusion.68
  154.0 59.3 %while.32 = (s32[]{:T(128)}, f32[10,24,1024]{2,1,0:T(8,128)}, s32[3328]{0:T(1024)S(1)}, s32[10]{0:T(128)S(1)}, f32[24,3328]{1,0:T(8,128)S(1)}, /*index=5*/s32[]{:T(128)}, s32[1]{0:T(128)}) while((s32[]{:T(128)}, f32[10,24,1024]{2,1,0:T(8,128)}, s32[3328]{0:T(1024)S(1)}, s32[10]{0:T(128)S(1)}, f32[24,3328]{1,0:T(8,128)S(1)}, ...), condition=%wide.region_5.6_spmd, body=%wide.region_4.5_spmd.sunk | while | flops 984876032 | bytes 439913 | solution.py:103
  155.3 4.7 %fusion.65 = f32[10,24,1024]{2,1,0:T(8,128)} fusion(f32[10,24,1024]{2,1,0:T(8,128)} %get-tuple-element.346, s32[]{:T(128)} %get-tuple-element.345, f32[24,3328]{1,0:T(8,128)S(1)} %get-tuple-element.356, s32[1024]{0:T(1024)S(1)} %iota_add_fusion.6, s32[3328]{0:T(1024)S(1)} %get-tuple-element.354), kind=kOutput, calls=%fused_computation.5.clone.1 | convolution fusion | flops 984875008 | bytes 435712 | tf_op jit(solution)/shard_map/while/body/eval_jaxpr/dot_general | solution.py:97
  161.2 4.7 %fusion.65 = f32[10,24,1024]{2,1,0:T(8,128)} fusion(f32[10,24,1024]{2,1,0:T(8,128)} %get-tuple-element.346, s32[]{:T(128)} %get-tuple-element.345, f32[24,3328]{1,0:T(8,128)S(1)} %get-tuple-element.356, s32[1024]{0:T(1024)S(1)} %iota_add_fusion.6, s32[3328]{0:T(1024)S(1)} %get-tuple-element.354), kind=kOutput, calls=%fused_computation.5.clone.1 | convolution fusion | flops 984875008 | bytes 435712 | tf_op jit(solution)/shard_map/while/body/eval_jaxpr/dot_general | solution.py:97
  167.2 4.7 %fusion.65 = f32[10,24,1024]{2,1,0:T(8,128)} fusion(f32[10,24,1024]{2,1,0:T(8,128)} %get-tuple-element.346, s32[]{:T(128)} %get-tuple-element.345, f32[24,3328]{1,0:T(8,128)S(1)} %get-tuple-element.356, s32[1024]{0:T(1024)S(1)} %iota_add_fusion.6, s32[3328]{0:T(1024)S(1)} %get-tuple-element.354), kind=kOutput, calls=%fused_computation.5.clone.1 | convolution fusion | flops 984875008 | bytes 435712 | tf_op jit(solution)/shard_map/while/body/eval_jaxpr/dot_general | solution.py:97
  173.1 4.7 %fusion.65 = f32[10,24,1024]{2,1,0:T(8,128)} fusion(f32[10,24,1024]{2,1,0:T(8,128)} %get-tuple-element.346, s32[]{:T(128)} %get-tuple-element.345, f32[24,3328]{1,0:T(8,128)S(1)} %get-tuple-element.356, s32[1024]{0:T(1024)S(1)} %iota_add_fusion.6, s32[3328]{0:T(1024)S(1)} %get-tuple-element.354), kind=kOutput, calls=%fused_computation.5.clone.1 | convolution fusion | flops 984875008 | bytes 435712 | tf_op jit(solution)/shard_map/while/body/eval_jaxpr/dot_general | solution.py:97
  179.0 4.7 %fusion.65 = f32[10,24,1024]{2,1,0:T(8,128)} fusion(f32[10,24,1024]{2,1,0:T(8,128)} %get-tuple-element.346, s32[]{:T(128)} %get-tuple-element.345, f32[24,3328]{1,0:T(8,128)S(1)} %get-tuple-element.356, s32[1024]{0:T(1024)S(1)} %iota_add_fusion.6, s32[3328]{0:T(1024)S(1)} %get-tuple-element.354), kind=kOutput, calls=%fused_computation.5.clone.1 | convolution fusion | flops 984875008 | bytes 435712 | tf_op jit(solution)/shard_map/while/body/eval_jaxpr/dot_general | solution.py:97
  184.9 4.7 %fusion.65 = f32[10,24,1024]{2,1,0:T(8,128)} fusion(f32[10,24,1024]{2,1,0:T(8,128)} %get-tuple-element.346, s32[]{:T(128)} %get-tuple-element.345, f32[24,3328]{1,0:T(8,128)S(1)} %get-tuple-element.356, s32[1024]{0:T(1024)S(1)} %iota_add_fusion.6, s32[3328]{0:T(1024)S(1)} %get-tuple-element.354), kind=kOutput, calls=%fused_computation.5.clone.1 | convolution fusion | flops 984875008 | bytes 435712 | tf_op jit(solution)/shard_map/while/body/eval_jaxpr/dot_general | solution.py:97
  190.9 4.7 %fusion.65 = f32[10,24,1024]{2,1,0:T(8,128)} fusion(f32[10,24,1024]{2,1,0:T(8,128)} %get-tuple-element.346, s32[]{:T(128)} %get-tuple-element.345, f32[24,3328]{1,0:T(8,128)S(1)} %get-tuple-element.356, s32[1024]{0:T(1024)S(1)} %iota_add_fusion.6, s32[3328]{0:T(1024)S(1)} %get-tuple-element.354), kind=kOutput, calls=%fused_computation.5.clone.1 | convolution fusion | flops 984875008 | bytes 435712 | tf_op jit(solution)/shard_map/while/body/eval_jaxpr/dot_general | solution.py:97
  196.8 4.7 %fusion.65 = f32[10,24,1024]{2,1,0:T(8,128)} fusion(f32[10,24,1024]{2,1,0:T(8,128)} %get-tuple-element.346, s32[]{:T(128)} %get-tuple-element.345, f32[24,3328]{1,0:T(8,128)S(1)} %get-tuple-element.356, s32[1024]{0:T(1024)S(1)} %iota_add_fusion.6, s32[3328]{0:T(1024)S(1)} %get-tuple-element.354), kind=kOutput, calls=%fused_computation.5.clone.1 | convolution fusion | flops 984875008 | bytes 435712 | tf_op jit(solution)/shard_map/while/body/eval_jaxpr/dot_general | solution.py:97
  202.7 4.7 %fusion.65 = f32[10,24,1024]{2,1,0:T(8,128)} fusion(f32[10,24,1024]{2,1,0:T(8,128)} %get-tuple-element.346, s32[]{:T(128)} %get-tuple-element.345, f32[24,3328]{1,0:T(8,128)S(1)} %get-tuple-element.356, s32[1024]{0:T(1024)S(1)} %iota_add_fusion.6, s32[3328]{0:T(1024)S(1)} %get-tuple-element.354), kind=kOutput, calls=%fused_computation.5.clone.1 | convolution fusion | flops 984875008 | bytes 435712 | tf_op jit(solution)/shard_map/while/body/eval_jaxpr/dot_general | solution.py:97
  208.7 4.7 %fusion.65 = f32[10,24,1024]{2,1,0:T(8,128)} fusion(f32[10,24,1024]{2,1,0:T(8,128)} %get-tuple-element.346, s32[]{:T(128)} %get-tuple-element.345, f32[24,3328]{1,0:T(8,128)S(1)} %get-tuple-element.356, s32[1024]{0:T(1024)S(1)} %iota_add_fusion.6, s32[3328]{0:T(1024)S(1)} %get-tuple-element.354), kind=kOutput, calls=%fused_computation.5.clone.1 | convolution fusion | flops 984875008 | bytes 435712 | tf_op jit(solution)/shard_map/while/body/eval_jaxpr/dot_general | solution.py:97
  216.6 4.0 %all-to-all-start = ((f32[8,8,3,1280]{3,1,2,0:T(8,128)}), f32[8,8,3,1280]{3,1,2,0:T(8,128)S(1)}, u32[]{:S(2)}, u32[]{:S(2)}) async-start(f32[8,8,3,1280]{3,1,2,0:T(8,128)} %copy.60), calls=%async_computation | async-start | bytes 1966080 | tf_op jit(solution)/shard_map/all_to_all | solution.py:39
  221.5 24.0 %all-to-all-done = f32[8,8,3,1280]{3,1,2,0:T(8,128)S(1)} async-done(((f32[8,8,3,1280]{3,1,2,0:T(8,128)}), f32[8,8,3,1280]{3,1,2,0:T(8,128)S(1)}, u32[]{:S(2)}, u32[]{:S(2)}) %all-to-all-start) | async-done | bytes 983072 | tf_op jit(solution)/shard_map/all_to_all | solution.py:39
  247.1 8.9 %all_to_all.17 = f32[8,1,32]{2,1,0:T(1,128)S(1)} all-to-all(f32[8,1,32]{2,1,0:T(1,128)S(1)} %broadcast_in_dim.14), channel_id=1, replica_groups=mesh['ctg'=32,'br'=8] {'br'}, dimensions={0} | all-to-all | bytes 2048 | tf_op jit(solution)/shard_map/all_to_all | solution.py:45
  256.9 16.7 %all_to_all.18 = f32[32,1,4]{2,1,0:T(1,128)S(1)} all-to-all(f32[32,1,4]{2,1,0:T(1,128)S(1)} %broadcast_in_dim.15), channel_id=1, replica_groups=mesh['ctg'=32,'br'=8] {'ctg'}, dimensions={0} | all-to-all | bytes 1024 | tf_op jit(solution)/shard_map/all_to_all | solution.py:45
  (145 shorter events, 64.2 us)
Async XLA Ops:
  7.2 71.0 %copy-start = (s32[8,1664]{1,0:T(8,128)S(1)}, s32[8,1664]{1,0:T(8,128)}, u32[]{:S(2)}) copy-start(s32[8,1664]{1,0:T(8,128)} %param.29) | copy-start | bytes 159748
  7.2 71.0 %copy-start.9 = (s32[1664]{0:T(1024)S(1)}, s32[1664]{0:T(1024)}, u32[]{:S(2)}) copy-start(s32[1664]{0:T(1024)} %param.28) | copy-start | bytes 19972
  7.2 71.0 %copy-start.10 = (s32[1664]{0:T(1024)S(1)}, s32[1664]{0:T(1024)}, u32[]{:S(2)}) copy-start(s32[1664]{0:T(1024)} %param.27) | copy-start | bytes 19972
  7.2 71.0 %copy-start.2 = (f32[1664]{0:T(1024)S(1)}, f32[1664]{0:T(1024)}, u32[]{:S(2)}) copy-start(f32[1664]{0:T(1024)} %param.31) | copy-start | bytes 19972
  7.2 71.0 %copy-start.8 = (f32[1664]{0:T(1024)S(1)}, f32[1664]{0:T(1024)}, u32[]{:S(2)}) copy-start(f32[1664]{0:T(1024)} %param.32) | copy-start | bytes 19972
  7.2 71.0 %all-gather.3.cloned.1.call-start = ((), (), s32[]{:S(2)}) async-start(), calls=%async_computation.3 | async-start | bytes 1474560 | tf_op jit(solution)/shard_map/all_gather | solution.py:24
  116.6 36.7 %copy-start.6 = (f32[1664]{0:T(1024)S(1)}, f32[1664]{0:T(1024)}, u32[]{:S(2)}) copy-start(f32[1664]{0:T(1024)} %param.30) | copy-start | bytes 19972
  216.6 4.0 %copy-start.7 = (f32[1664]{0:T(1024)S(1)}, f32[1664]{0:T(1024)}, u32[]{:S(2)}) copy-start(f32[1664]{0:T(1024)} %param.33) | copy-start | bytes 19972
  216.6 4.1 %copy-start.3 = (f32[8,1664]{1,0:T(8,128)S(1)}, f32[8,1664]{1,0:T(8,128)}, u32[]{:S(2)}) copy-start(f32[8,1664]{1,0:T(8,128)} %param.34) | copy-start | bytes 159748
  216.6 4.1 %copy-start.4 = (f32[8,1664]{1,0:T(8,128)S(1)}, f32[8,1664]{1,0:T(8,128)}, u32[]{:S(2)}) copy-start(f32[8,1664]{1,0:T(8,128)} %param.35) | copy-start | bytes 159748
  216.6 29.0 %copy-start.5 = (f32[8,1280]{1,0:T(8,128)S(1)}, f32[8,1280]{1,0:T(8,128)}, u32[]{:S(2)}) copy-start(f32[8,1280]{1,0:T(8,128)} %param.26) | copy-start | bytes 122884
  216.6 28.9 %all-to-all-start = ((f32[8,8,3,1280]{3,1,2,0:T(8,128)}), f32[8,8,3,1280]{3,1,2,0:T(8,128)S(1)}, u32[]{:S(2)}, u32[]{:S(2)}) async-start(f32[8,8,3,1280]{3,1,2,0:T(8,128)} %copy.60), calls=%async_computation | async-start | bytes 1966080 | tf_op jit(solution)/shard_map/all_to_all | solution.py:39
  220.7 25.7 %copy-start.1 = (f32[8,2,1280]{2,1,0:T(2,128)S(1)}, f32[8,2,1280]{2,1,0:T(2,128)}, u32[]{:S(2)}) copy-start(f32[8,2,1280]{2,1,0:T(2,128)} %param.25) | copy-start | bytes 245764
Sparse Core Ops, SparseCore 0:
  9.9 38.6 all-gather.2
where the time goes:
time: 283 us; the launch traced here: 281 us
  matrix products  94.7 us (33%)
  blocking collectives  92.8 us (33%)
  local copies, waits for them, and re-layouts  24.9 us (9%)
  waiting for transfers between devices  24.1 us (9%)
  loops' own time  20.3 us (7%)
  between operations  14.4 us (5%)
  other arithmetic  5.73 us (2%)
  starting transfers between devices  4.05 us (1%)
    all_gather x1, blocking collectives, turned_gather(): whole = lax.all_gather(both, axis, axis=0, tiled=True)  67.2 us
    dot_general x20, matrix products, add_block(): jnp.dot(segment, onehot, precision=lax.Precision.HIGHEST, preferred_eleme...  47.9 us
    dot_general x10, matrix products, one_block(): jnp.dot(values, onehot, precision=lax.Precision.HIGHEST, preferred_elemen...  46.8 us
    all_to_all x2, blocking collectives, sent_to_all(): return lax.all_to_all(copies, axis, split_axis=0, concat_axis=0, tiled=True)  25.6 us
    all_to_all x1, waiting for transfers between devices, summed_on_arrival(): lax.all_to_all(in_blocks(array, dim, peers), axis, 0, 0, tiled=True)  24 us
    dynamic_slice x30, local copies, waits for them, and re-layouts, select_cols(): result, _ = lax.scan(add_block, start_zero, (tiles, numbers))  17.6 us
    another operation x2, loops' own time, select_cols(): result, _ = lax.scan(add_block, start_zero, (tiles, numbers))  13.7 us
    another operation x1, loops' own time, spread_rows(): _, pieces = lax.scan(one_block, jnp.int32(0), numbers)  6.61 us
  transfers between devices with their start and end apart: 2, of which 1 were waited for; matrix products, arithmetic and copies ran while one was open for 1% of the time, Pallas kernels for 0%

commit v1 on v0

--- a/solution.py
+++ b/solution.py
@@ -9,7 +9,9 @@
     turned = [jnp.moveaxis(a, dim, 0) for a, dim in zip(arrays, dims)]
     widths = [t[0].size for t in turned]
     both = jnp.concatenate([t.reshape(-1, w) for t, w in zip(turned, widths)], axis=1)
-    whole = lax.all_gather(both, axis, axis=0, tiled=True)
+    whole = jnp.concatenate(
+        lax.all_to_all(jnp.stack([both] * lax.axis_size(axis)), axis, 0, 0), axis=0
+    )
     pieces = jnp.split(whole, [sum(widths[:k]) for k in range(1, len(widths))], axis=1)
     return tuple(
         (

time: 283 us -> 257 us (0.908)
  blocking collectives: 92.8 us -> 27.8 us
  waiting for transfers between devices: 24.1 us -> 47.5 us
  starting transfers between devices: 4.05 us -> 19.7 us
    all_gather x1 -> x0, blocking collectives: 67.2 us -> none  [turned_gather(): whole = lax.all_gather(both, axis, axis=0, tiled=True)]
    all_to_all x0 -> x1, waiting for transfers between devices: none -> 18.3 us  [turned_gather(): lax.all_to_all(jnp.stack([both] * lax.axis_size(axis)), axis, 0, 0)]
    all_to_all x0 -> x1, starting transfers between devices: none -> 15.6 us  [turned_gather(): lax.all_to_all(jnp.stack([both] * lax.axis_size(axis)), axis, 0, 0)]
    all_gather x1, waiting for transfers between devices: 0.02 us -> 5.84 us  [in_one_piece(): lax.all_gather(both, axis, axis=dim, tiled=True)]
  transfers between devices with their start and end apart: 2 -> 3, of which waited for: 1 -> 3; matrix products, arithmetic and copies ran while one was open for 1% -> 1% of each run, Pallas kernels for 0% -> 0%
where the time goes in v1:
time: 257 us; the launch traced here: 256 us
  matrix products  94.8 us (37%)
  waiting for transfers between devices  47.5 us (18%)
  blocking collectives  27.8 us (11%)
  local copies, waits for them, and re-layouts  25.7 us (10%)
  loops' own time  20.3 us (8%)
  starting transfers between devices  19.7 us (8%)
  between operations  14.4 us (6%)
  other arithmetic  5.66 us (2%)
    dot_general x20, matrix products, add_block(): jnp.dot(segment, onehot, precision=lax.Precision.HIGHEST, preferred_eleme...  47.9 us
    dot_general x10, matrix products, one_block(): jnp.dot(values, onehot, precision=lax.Precision.HIGHEST, preferred_elemen...  46.9 us
    all_to_all x2, blocking collectives, sent_to_all(): return lax.all_to_all(copies, axis, split_axis=0, concat_axis=0, tiled=True)  27.8 us
    all_to_all x1, waiting for transfers between devices, summed_on_arrival(): lax.all_to_all(in_blocks(array, dim, peers), axis, 0, 0, tiled=True)  23.4 us
    all_to_all x1, waiting for transfers between devices, turned_gather(): lax.all_to_all(jnp.stack([both] * lax.axis_size(axis)), axis, 0, 0)  18.3 us
    dynamic_slice x30, local copies, waits for them, and re-layouts, select_cols(): result, _ = lax.scan(add_block, start_zero, (tiles, numbers))  17.6 us
    all_to_all x1, starting transfers between devices, turned_gather(): lax.all_to_all(jnp.stack([both] * lax.axis_size(axis)), axis, 0, 0)  15.6 us
    another operation x2, loops' own time, select_cols(): result, _ = lax.scan(add_block, start_zero, (tiles, numbers))  13.7 us
  transfers between devices with their start and end apart: 3, of which 3 were waited for; matrix products, arithmetic and copies ran while one was open for 1% of the time, Pallas kernels for 0%

profile of v1, /device:TPU:1, one launch (start us, length us, event | category | flops | bytes accessed | tf_op | source)
XLA Modules:
  0.0 255.8 jit_solution(12255671352523223641)
XLA Ops:
  11.2 15.6 %all-to-all-start = ((f32[256,40,2]{1,2,0:T(2,128)}), f32[256,40,2]{1,2,0:T(2,128)S(1)}, u32[]{:S(2)}, u32[]{:S(2)}) async-start(f32[256,40,2]{1,2,0:T(2,128)} %stack.28), calls=%async_computation | async-start | bytes 524288 | tf_op jit(solution)/shard_map/all_to_all | solution.py:13
  27.0 18.3 %all-to-all-done = f32[256,40,2]{1,2,0:T(2,128)S(1)} async-done(((f32[256,40,2]{1,2,0:T(2,128)}), f32[256,40,2]{1,2,0:T(2,128)S(1)}, u32[]{:S(2)}, u32[]{:S(2)}) %all-to-all-start) | async-done | bytes 81952 | tf_op jit(solution)/shard_map/all_to_all | solution.py:13
  45.7 5.8 %all-gather.2.cloned.1.call-done = f32[16,2,10240]{2,0,1:T(8,128)} async-done(((f32[16,2,1280]{2,0,1:T(8,128)}), f32[16,2,10240]{2,0,1:T(8,128)}) %all-gather.2.cloned.1.call-update) | async-done | bytes 1310736 | tf_op jit(solution)/shard_map/all_gather | solution.py:26
  53.1 36.7 %while.34 = (s32[]{:T(128)}, f32[32,1664]{1,0:T(8,128)S(1)}, f32[10,32,1024]{2,1,0:T(8,128)S(1)}, s32[10]{0:T(128)S(1)}, s32[1664]{0:T(1024)S(1)}, /*index=5*/s32[]{:T(128)}, s32[1]{0:T(128)}, s32[]{:T(128)}) while((s32[]{:T(128)}, f32[32,1664]{1,0:T(8,128)S(1)}, f32[10,32,1024]{2,1,0:T(8,128)S(1)}, s32[10]{0:T(128)S(1)}, ...), condition=%wide.region_3.4_spmd.clone, body=%wide.region_2.3_spmd.clone.sunk | while | flops 656122880 | bytes 573567 | solution.py:87
  54.4 2.4 fusion.71
  58.0 2.4 fusion.71
  61.7 2.4 fusion.71
  65.4 2.4 fusion.71
  89.8 36.7 %while.33 = (s32[]{:T(128)}, f32[32,1664]{1,0:T(8,128)S(1)}, f32[10,32,1024]{2,1,0:T(8,128)S(1)}, s32[10]{0:T(128)S(1)}, s32[1664]{0:T(1024)S(1)}, /*index=5*/s32[]{:T(128)}, s32[1]{0:T(128)}, s32[]{:T(128)}) while((s32[]{:T(128)}, f32[32,1664]{1,0:T(8,128)S(1)}, f32[10,32,1024]{2,1,0:T(8,128)S(1)}, s32[10]{0:T(128)S(1)}, ...), condition=%wide.region_1.2_spmd.clone, body=%wide.region_0.1_spmd.clone.sunk | while | flops 656122880 | bytes 573567 | solution.py:87
  127.3 59.3 %while.32 = (s32[]{:T(128)}, f32[10,24,1024]{2,1,0:T(8,128)}, s32[3328]{0:T(1024)S(1)}, s32[10]{0:T(128)S(1)}, f32[24,3328]{1,0:T(8,128)S(1)}, /*index=5*/s32[]{:T(128)}, s32[1]{0:T(128)}) while((s32[]{:T(128)}, f32[10,24,1024]{2,1,0:T(8,128)}, s32[3328]{0:T(1024)S(1)}, s32[10]{0:T(128)S(1)}, f32[24,3328]{1,0:T(8,128)S(1)}, ...), condition=%wide.region_5.6_spmd, body=%wide.region_4.5_spmd.sunk | while | flops 984876032 | bytes 439913 | solution.py:105
  128.5 4.7 %fusion.65 = f32[10,24,1024]{2,1,0:T(8,128)} fusion(f32[10,24,1024]{2,1,0:T(8,128)} %get-tuple-element.346, s32[]{:T(128)} %get-tuple-element.345, f32[24,3328]{1,0:T(8,128)S(1)} %get-tuple-element.356, s32[1024]{0:T(1024)S(1)} %iota_add_fusion.6, s32[3328]{0:T(1024)S(1)} %get-tuple-element.354), kind=kOutput, calls=%fused_computation.5.clone.1 | convolution fusion | flops 984875008 | bytes 435712 | tf_op jit(solution)/shard_map/while/body/eval_jaxpr/dot_general | solution.py:99
  134.5 4.7 %fusion.65 = f32[10,24,1024]{2,1,0:T(8,128)} fusion(f32[10,24,1024]{2,1,0:T(8,128)} %get-tuple-element.346, s32[]{:T(128)} %get-tuple-element.345, f32[24,3328]{1,0:T(8,128)S(1)} %get-tuple-element.356, s32[1024]{0:T(1024)S(1)} %iota_add_fusion.6, s32[3328]{0:T(1024)S(1)} %get-tuple-element.354), kind=kOutput, calls=%fused_computation.5.clone.1 | convolution fusion | flops 984875008 | bytes 435712 | tf_op jit(solution)/shard_map/while/body/eval_jaxpr/dot_general | solution.py:99
  140.4 4.7 %fusion.65 = f32[10,24,1024]{2,1,0:T(8,128)} fusion(f32[10,24,1024]{2,1,0:T(8,128)} %get-tuple-element.346, s32[]{:T(128)} %get-tuple-element.345, f32[24,3328]{1,0:T(8,128)S(1)} %get-tuple-element.356, s32[1024]{0:T(1024)S(1)} %iota_add_fusion.6, s32[3328]{0:T(1024)S(1)} %get-tuple-element.354), kind=kOutput, calls=%fused_computation.5.clone.1 | convolution fusion | flops 984875008 | bytes 435712 | tf_op jit(solution)/shard_map/while/body/eval_jaxpr/dot_general | solution.py:99
  146.3 4.7 %fusion.65 = f32[10,24,1024]{2,1,0:T(8,128)} fusion(f32[10,24,1024]{2,1,0:T(8,128)} %get-tuple-element.346, s32[]{:T(128)} %get-tuple-element.345, f32[24,3328]{1,0:T(8,128)S(1)} %get-tuple-element.356, s32[1024]{0:T(1024)S(1)} %iota_add_fusion.6, s32[3328]{0:T(1024)S(1)} %get-tuple-element.354), kind=kOutput, calls=%fused_computation.5.clone.1 | convolution fusion | flops 984875008 | bytes 435712 | tf_op jit(solution)/shard_map/while/body/eval_jaxpr/dot_general | solution.py:99
  152.2 4.7 %fusion.65 = f32[10,24,1024]{2,1,0:T(8,128)} fusion(f32[10,24,1024]{2,1,0:T(8,128)} %get-tuple-element.346, s32[]{:T(128)} %get-tuple-element.345, f32[24,3328]{1,0:T(8,128)S(1)} %get-tuple-element.356, s32[1024]{0:T(1024)S(1)} %iota_add_fusion.6, s32[3328]{0:T(1024)S(1)} %get-tuple-element.354), kind=kOutput, calls=%fused_computation.5.clone.1 | convolution fusion | flops 984875008 | bytes 435712 | tf_op jit(solution)/shard_map/while/body/eval_jaxpr/dot_general | solution.py:99
  158.2 4.7 %fusion.65 = f32[10,24,1024]{2,1,0:T(8,128)} fusion(f32[10,24,1024]{2,1,0:T(8,128)} %get-tuple-element.346, s32[]{:T(128)} %get-tuple-element.345, f32[24,3328]{1,0:T(8,128)S(1)} %get-tuple-element.356, s32[1024]{0:T(1024)S(1)} %iota_add_fusion.6, s32[3328]{0:T(1024)S(1)} %get-tuple-element.354), kind=kOutput, calls=%fused_computation.5.clone.1 | convolution fusion | flops 984875008 | bytes 435712 | tf_op jit(solution)/shard_map/while/body/eval_jaxpr/dot_general | solution.py:99
  164.1 4.7 %fusion.65 = f32[10,24,1024]{2,1,0:T(8,128)} fusion(f32[10,24,1024]{2,1,0:T(8,128)} %get-tuple-element.346, s32[]{:T(128)} %get-tuple-element.345, f32[24,3328]{1,0:T(8,128)S(1)} %get-tuple-element.356, s32[1024]{0:T(1024)S(1)} %iota_add_fusion.6, s32[3328]{0:T(1024)S(1)} %get-tuple-element.354), kind=kOutput, calls=%fused_computation.5.clone.1 | convolution fusion | flops 984875008 | bytes 435712 | tf_op jit(solution)/shard_map/while/body/eval_jaxpr/dot_general | solution.py:99
  170.0 4.7 %fusion.65 = f32[10,24,1024]{2,1,0:T(8,128)} fusion(f32[10,24,1024]{2,1,0:T(8,128)} %get-tuple-element.346, s32[]{:T(128)} %get-tuple-element.345, f32[24,3328]{1,0:T(8,128)S(1)} %get-tuple-element.356, s32[1024]{0:T(1024)S(1)} %iota_add_fusion.6, s32[3328]{0:T(1024)S(1)} %get-tuple-element.354), kind=kOutput, calls=%fused_computation.5.clone.1 | convolution fusion | flops 984875008 | bytes 435712 | tf_op jit(solution)/shard_map/while/body/eval_jaxpr/dot_general | solution.py:99
  176.0 4.7 %fusion.65 = f32[10,24,1024]{2,1,0:T(8,128)} fusion(f32[10,24,1024]{2,1,0:T(8,128)} %get-tuple-element.346, s32[]{:T(128)} %get-tuple-element.345, f32[24,3328]{1,0:T(8,128)S(1)} %get-tuple-element.356, s32[1024]{0:T(1024)S(1)} %iota_add_fusion.6, s32[3328]{0:T(1024)S(1)} %get-tuple-element.354), kind=kOutput, calls=%fused_computation.5.clone.1 | convolution fusion | flops 984875008 | bytes 435712 | tf_op jit(solution)/shard_map/while/body/eval_jaxpr/dot_general | solution.py:99
  181.9 4.7 %fusion.65 = f32[10,24,1024]{2,1,0:T(8,128)} fusion(f32[10,24,1024]{2,1,0:T(8,128)} %get-tuple-element.346, s32[]{:T(128)} %get-tuple-element.345, f32[24,3328]{1,0:T(8,128)S(1)} %get-tuple-element.356, s32[1024]{0:T(1024)S(1)} %iota_add_fusion.6, s32[3328]{0:T(1024)S(1)} %get-tuple-element.354), kind=kOutput, calls=%fused_computation.5.clone.1 | convolution fusion | flops 984875008 | bytes 435712 | tf_op jit(solution)/shard_map/while/body/eval_jaxpr/dot_general | solution.py:99
  189.9 4.0 %all-to-all-start.1 = ((f32[8,8,3,1280]{3,1,2,0:T(8,128)}), f32[8,8,3,1280]{3,1,2,0:T(8,128)S(1)}, u32[]{:S(2)}, u32[]{:S(2)}) async-start(f32[8,8,3,1280]{3,1,2,0:T(8,128)} %copy.59), calls=%async_computation.1 | async-start | bytes 1966080 | tf_op jit(solution)/shard_map/all_to_all | solution.py:41
  194.8 23.4 %all-to-all-done.1 = f32[8,8,3,1280]{3,1,2,0:T(8,128)S(1)} async-done(((f32[8,8,3,1280]{3,1,2,0:T(8,128)}), f32[8,8,3,1280]{3,1,2,0:T(8,128)S(1)}, u32[]{:S(2)}, u32[]{:S(2)}) %all-to-all-start.1) | async-done | bytes 983072 | tf_op jit(solution)/shard_map/all_to_all | solution.py:41
  219.8 8.9 %all_to_all.22 = f32[8,1,32]{2,1,0:T(1,128)S(1)} all-to-all(f32[8,1,32]{2,1,0:T(1,128)S(1)} %broadcast_in_dim.14), channel_id=1, replica_groups=mesh['ctg'=32,'br'=8] {'br'}, dimensions={0} | all-to-all | bytes 2048 | tf_op jit(solution)/shard_map/all_to_all | solution.py:47
  229.5 18.9 %all_to_all.23 = f32[32,1,4]{2,1,0:T(1,128)S(1)} all-to-all(f32[32,1,4]{2,1,0:T(1,128)S(1)} %broadcast_in_dim.15), channel_id=1, replica_groups=mesh['ctg'=32,'br'=8] {'ctg'}, dimensions={0} | all-to-all | bytes 1024 | tf_op jit(solution)/shard_map/all_to_all | solution.py:47
  (147 shorter events, 69.7 us)
Async XLA Ops:
  7.2 19.7 %copy-start.2 = (f32[1664]{0:T(1024)S(1)}, f32[1664]{0:T(1024)}, u32[]{:S(2)}) copy-start(f32[1664]{0:T(1024)} %param.31) | copy-start | bytes 19972
  7.2 19.7 %copy-start.8 = (f32[1664]{0:T(1024)S(1)}, f32[1664]{0:T(1024)}, u32[]{:S(2)}) copy-start(f32[1664]{0:T(1024)} %param.32) | copy-start | bytes 19972
  7.2 19.7 %copy-start = (s32[8,1664]{1,0:T(8,128)S(1)}, s32[8,1664]{1,0:T(8,128)}, u32[]{:S(2)}) copy-start(s32[8,1664]{1,0:T(8,128)} %param.29) | copy-start | bytes 159748
  7.2 19.7 %copy-start.9 = (s32[1664]{0:T(1024)S(1)}, s32[1664]{0:T(1024)}, u32[]{:S(2)}) copy-start(s32[1664]{0:T(1024)} %param.28) | copy-start | bytes 19972
  7.2 19.7 %copy-start.10 = (s32[1664]{0:T(1024)S(1)}, s32[1664]{0:T(1024)}, u32[]{:S(2)}) copy-start(s32[1664]{0:T(1024)} %param.27) | copy-start | bytes 19972
  7.2 44.3 %all-gather.2.cloned.1.call-start = ((), (), s32[]{:S(2)}) async-start(), calls=%async_computation.4 | async-start | bytes 1474560 | tf_op jit(solution)/shard_map/all_gather | solution.py:26
  11.2 34.0 %all-to-all-start = ((f32[256,40,2]{1,2,0:T(2,128)}), f32[256,40,2]{1,2,0:T(2,128)S(1)}, u32[]{:S(2)}, u32[]{:S(2)}) async-start(f32[256,40,2]{1,2,0:T(2,128)} %stack.28), calls=%async_computation | async-start | bytes 524288 | tf_op jit(solution)/shard_map/all_to_all | solution.py:13
  89.8 36.7 %copy-start.6 = (f32[1664]{0:T(1024)S(1)}, f32[1664]{0:T(1024)}, u32[]{:S(2)}) copy-start(f32[1664]{0:T(1024)} %param.30) | copy-start | bytes 19972
  189.9 4.0 %copy-start.7 = (f32[1664]{0:T(1024)S(1)}, f32[1664]{0:T(1024)}, u32[]{:S(2)}) copy-start(f32[1664]{0:T(1024)} %param.33) | copy-start | bytes 19972
  189.9 4.1 %copy-start.3 = (f32[8,1664]{1,0:T(8,128)S(1)}, f32[8,1664]{1,0:T(8,128)}, u32[]{:S(2)}) copy-start(f32[8,1664]{1,0:T(8,128)} %param.34) | copy-start | bytes 159748
  189.9 4.1 %copy-start.4 = (f32[8,1664]{1,0:T(8,128)S(1)}, f32[8,1664]{1,0:T(8,128)}, u32[]{:S(2)}) copy-start(f32[8,1664]{1,0:T(8,128)} %param.35) | copy-start | bytes 159748
  189.9 28.3 %copy-start.5 = (f32[8,1280]{1,0:T(8,128)S(1)}, f32[8,1280]{1,0:T(8,128)}, u32[]{:S(2)}) copy-start(f32[8,1280]{1,0:T(8,128)} %param.26) | copy-start | bytes 122884
  189.9 28.2 %all-to-all-start.1 = ((f32[8,8,3,1280]{3,1,2,0:T(8,128)}), f32[8,8,3,1280]{3,1,2,0:T(8,128)S(1)}, u32[]{:S(2)}, u32[]{:S(2)}) async-start(f32[8,8,3,1280]{3,1,2,0:T(8,128)} %copy.59), calls=%async_computation.1 | async-start | bytes 1966080 | tf_op jit(solution)/shard_map/all_to_all | solution.py:41
  193.9 25.0 %copy-start.1 = (f32[8,2,1280]{2,1,0:T(2,128)S(1)}, f32[8,2,1280]{2,1,0:T(2,128)}, u32[]{:S(2)}) copy-start(f32[8,2,1280]{2,1,0:T(2,128)} %param.25) | copy-start | bytes 245764
Sparse Core Ops, SparseCore 0:
  9.9 41.6 all-gather.1
